TPU v7x, 32 devices: a whole 2x2x4 slice. The times are simulated.
32 devices in a mesh: grp: 2 (over y), row: 16 (over z, x, core).
Axes of the slice: x: 2, y: 2, z: 4, core: 2. Of those that a mesh axis runs over, the one named last changes fastest.
Arguments:
- item_ids: int32 [128, 512], P(('grp', 'row')), may hold values from 0 to 49999, as said below
- lengths: int32 [128], P(('grp', 'row')), may hold values from 358 to 512
- target_ids: int32 [128, 512], P(('grp', 'row')), may hold values from 0 to 49999
- target_logq: bfloat16 [128, 512], P(('grp', 'row')), may hold values from -4 to 0
- negative_ids: int32 [2048], P(('grp', 'row')), may hold values from 0 to 49999
- negative_logq: bfloat16 [2048], P(('grp', 'row')), may hold values from -4 to 0
- table_weight: float32 [50000, 256], P('row'), may hold values from -0.6 to 0.6
- table_accum: float32 [50000], P('row'), may hold values from 1.1737531e-13 to 4.6950123e-13
- dense_weight: float32 [256, 4608], P(None, ('grp', 'row')), may hold values from -0.375 to 0.375
- dense_first: float32 [256, 4608], P(None, ('grp', 'row')), may hold values from -2.861023e-06 to 2.861023e-06
- dense_second: float32 [256, 4608], P(None, ('grp', 'row')), may hold values from 3.390842e-15 to 1.3563368e-14
- gain_weight: float32 [3, 256], replicated, may hold values from 0.5 to 1.5
- gain_first: float32 [3, 256], replicated, may hold values from -3.0517578e-05 to 3.0517578e-05
- gain_second: float32 [3, 256], replicated, may hold values from 3.390842e-13 to 1.3563368e-12
Outputs:
- mean_loss: float32 [], replicated
- grad_norm: float32 [], replicated
- new_table: float32 [50000, 256], P('row')
- table_grad: float32 [50000, 256], P('row')
- new_accum: float32 [50000], P('row')
- table_copy: bfloat16 [50000, 256], P('row')
- new_dense: float32 [256, 4608], P(None, ('grp', 'row'))
- new_first: float32 [256, 4608], P(None, ('grp', 'row'))
- new_second: float32 [256, 4608], P(None, ('grp', 'row'))
- dense_copy: bfloat16 [256, 4608], P(None, ('grp', 'row'))
- new_gains: float32 [3, 256], replicated
- new_gain_first: float32 [3, 256], replicated
- new_gain_second: float32 [3, 256], replicated
Inputs may be any that keep to these rules, and one draw needn't show every extreme that they name: `item_ids`: taking one device's item ids, target ids and negative ids together, at most 520 of them name rows with the same id // 3125; in each group some value of id // 3125 is named exactly 520 times by every device of the group.
All inputs are finite; a program needn't handle non-finite values.
Results may differ from a plain program's by a relative error of at most 0.0093.
The roundings to bfloat16 on the way count: a program that leaves them out, or rounds other values in their place, can miss the bound.
Values may be sent and summed in bfloat16 or wider, within the bound.
A program may use at most 256 MiB of HBM per device.

v0:
```python
import jax
import jax.numpy as jnp
from jax import lax
from jax.sharding import PartitionSpec as P

HEADS = 8
HDIM = 64
FF = 1024
STEP = 10
clip_level = 0.002
adam_rate = 0.05
gains_rate = 0.6
rows_rate = 0.05
beta_one = 0.9
beta_two = 0.999
adam_eps = 1e-08
decay_rate = 0.01


def in_blocks(array, dim, devices):
    shape = array.shape
    pieces = array.reshape(*shape[:dim], devices, shape[dim] // devices, *shape[dim + 1 :])
    return jnp.moveaxis(pieces, dim, 0)


def sum_at_owner(array, axis, dim):
    devices = lax.axis_size(axis)
    pieces = lax.all_to_all(in_blocks(array, dim, devices), axis, 0, 0, tiled=True)
    return jnp.sum(pieces.astype(jnp.float32), axis=0)


def norm_apply(values, gain):
    return values * lax.rsqrt(jnp.mean(values * values, -1, keepdims=True) + 1e-06) * gain


def gelu_apply(values):
    return jax.nn.gelu(values, approximate=True)


def adam_update(weight, first, second, grad, decay, rate):
    first_new = beta_one * first + (1.0 - beta_one) * grad
    second_new = beta_two * second + (1.0 - beta_two) * grad * grad
    fix_one = 1.0 - beta_one**STEP
    fix_two = 1.0 - beta_two**STEP
    weight_new = weight - rate * (
        first_new / fix_one / (jnp.sqrt(second_new / fix_two) + adam_eps) + decay * weight
    )
    return (weight_new, first_new, second_new)


def attention_probs(queries, keys_all):
    scores = (
        jnp.einsum("sqhd,skhd->shqk", queries, keys_all, preferred_element_type=jnp.float32) * 0.125
    )
    length = queries.shape[1]
    causal = lax.broadcasted_iota(jnp.int32, (length, length), 0) >= lax.broadcasted_iota(
        jnp.int32, (length, length), 1
    )
    scores = jnp.where(causal[None, None], scores, -1e30)
    exponent = jnp.exp(scores - jnp.max(scores, -1, keepdims=True))
    return exponent / jnp.sum(exponent, -1, keepdims=True)


def shards(
    item_ids,
    lengths,
    target_ids,
    target_logq,
    negative_ids,
    negative_logq,
    table_weight,
    table_accum,
    dense_weight,
    dense_first,
    dense_second,
    gain_weight,
    gain_first,
    gain_second,
):
    seq_dev, length = item_ids.shape
    rows_dev, model_width = table_weight.shape
    peer_count = lax.axis_size("row")
    inner = HEADS * HDIM
    tokens = seq_dev * length
    single_float = jnp.float32
    brain_float_half = jnp.bfloat16
    local_dense = dense_weight.astype(brain_float_half)
    full_dense = lax.all_gather(local_dense, ("grp", "row"), axis=1, tiled=True)
    query_key_value_weight = full_dense[:, : 3 * inner]
    output_weight = full_dense[:, 3 * inner : 4 * inner]
    up_weight = full_dense[:, 4 * inner : 4 * inner + FF]
    down_weight = full_dense[:, 4 * inner + FF : 4 * inner + 2 * FF]
    pos_rows = full_dense[:, 4 * inner + 2 * FF :].T.astype(single_float)
    requests = jnp.concatenate([item_ids.reshape(-1), target_ids.reshape(-1), negative_ids])
    capacity = 2 * requests.shape[0] // peer_count
    owners = requests // rows_dev
    one_hot = (owners[:, None] == jnp.arange(peer_count, dtype=jnp.int32)[None, :]).astype(
        jnp.int32
    )
    rank_in = jnp.sum((jnp.cumsum(one_hot, 0) - one_hot) * one_hot, 1)
    slot_at = owners * capacity + rank_in
    send_ids = jnp.full((peer_count * capacity,), -1, jnp.int32).at[slot_at].set(requests)
    send_ids = send_ids.reshape(peer_count, capacity)
    table_low = table_weight.astype(brain_float_half)
    row_base = lax.axis_index("row") * rows_dev
    asked_ids = lax.all_to_all(send_ids, "row", split_axis=0, concat_axis=0, tiled=True)
    present = asked_ids >= 0
    found_rows = table_low[jnp.where(present, asked_ids - row_base, 0)]
    found_rows = jnp.where(present[..., None], found_rows, jnp.zeros_like(found_rows))
    returned = lax.all_to_all(found_rows, "row", split_axis=0, concat_axis=0, tiled=True)
    fetched, asked_ids = (returned, asked_ids)
    picked = fetched.reshape(peer_count * capacity, model_width)[slot_at]
    hist_rows = picked[:tokens].reshape(seq_dev, length, model_width)
    target_rows = picked[tokens : 2 * tokens]
    own_negatives = picked[2 * tokens :]
    neg_rows, neg_bias = (
        lax.all_gather(own_negatives, "row", axis=0, tiled=True),
        lax.all_gather(negative_logq, "row", axis=0, tiled=True),
    )
    embedded_tokens = hist_rows.astype(single_float) + pos_rows[None]
    normed, norm_back_one = jax.vjp(norm_apply, embedded_tokens, gain_weight[0])
    normalized_narrow = normed.astype(brain_float_half)
    mixed_state = jnp.einsum(
        "rnq,qm->rnm",
        normalized_narrow,
        query_key_value_weight,
        preferred_element_type=single_float,
    ).astype(brain_float_half)
    queries = mixed_state[..., :inner].reshape(seq_dev, length, HEADS, HDIM)
    keys_all = mixed_state[..., inner : 2 * inner].reshape(seq_dev, length, HEADS, HDIM)
    values_all = mixed_state[..., 2 * inner :].reshape(seq_dev, length, HEADS, HDIM)
    attn_probs = attention_probs(queries, keys_all)
    probs_low = attn_probs.astype(brain_float_half)
    attention_context = jnp.einsum(
        "shqk,skhd->sqhd", probs_low, values_all, preferred_element_type=single_float
    )
    attention_context = attention_context.reshape(seq_dev, length, inner).astype(brain_float_half)
    after_attention_state = embedded_tokens + jnp.einsum(
        "xaj,oj->xao", attention_context, output_weight, preferred_element_type=single_float
    )
    normed_two, norm_back_two = jax.vjp(norm_apply, after_attention_state, gain_weight[1])
    second_normalized_narrow = normed_two.astype(brain_float_half)
    hidden_preactivation = jnp.einsum(
        "bvi,iq->bvq", second_normalized_narrow, up_weight, preferred_element_type=single_float
    )
    hidden, gaussian_unit_backward = jax.vjp(gelu_apply, hidden_preactivation)
    hidden_narrow = hidden.astype(brain_float_half)
    after_ffn = after_attention_state + jnp.einsum(
        "ixn,on->ixo", hidden_narrow, down_weight, preferred_element_type=single_float
    )
    states, norm_back_three = jax.vjp(norm_apply, after_ffn, gain_weight[2])
    states_low = states.astype(brain_float_half).reshape(tokens, model_width)
    states_full = states_low.astype(single_float)
    target_full = target_rows.astype(single_float)
    pos_logit = jnp.sum(states_full * target_full, -1) - target_logq.reshape(tokens).astype(
        single_float
    )
    neg_logit = (
        jnp.einsum("td,nd->tn", states_low, neg_rows, preferred_element_type=single_float)
        - neg_bias.astype(single_float)[None, :]
    )
    highest_logit = jnp.maximum(jnp.max(neg_logit, 1), pos_logit)
    log_total = highest_logit + jnp.log(
        jnp.exp(pos_logit - highest_logit) + jnp.sum(jnp.exp(neg_logit - highest_logit[:, None]), 1)
    )
    is_valid = lax.broadcasted_iota(jnp.int32, (seq_dev, length), 1) < lengths[:, None]
    valid_full = is_valid.reshape(tokens).astype(single_float)
    loss_local = jnp.sum(valid_full * (log_total - pos_logit))
    event_local = jnp.sum(valid_full)
    loss_total, event_total = lax.psum((loss_local, event_local), ("grp", "row"))
    inverse = 1.0 / event_total
    d_pos = valid_full * inverse * (jnp.exp(pos_logit - log_total) - 1.0)
    d_neg = (valid_full[:, None] * inverse * jnp.exp(neg_logit - log_total[:, None])).astype(
        brain_float_half
    )
    d_states = d_pos[:, None] * target_full + jnp.einsum(
        "tn,nd->td", d_neg, neg_rows, preferred_element_type=single_float
    )
    d_target = d_pos[:, None] * states_full
    neg_grad = sum_at_owner(
        jnp.einsum("tn,td->nd", d_neg, states_low, preferred_element_type=single_float).astype(
            jnp.bfloat16
        ),
        "row",
        0,
    )
    d_ffn, d_gain_three = norm_back_three(d_states.reshape(seq_dev, length, model_width))
    branch_gradient = d_ffn.astype(brain_float_half)
    down_weight_gradient = jnp.einsum(
        "qgp,qgv->pv", branch_gradient, hidden_narrow, preferred_element_type=single_float
    )
    (hidden_gradient,) = gaussian_unit_backward(
        jnp.einsum("bvi,iq->bvq", branch_gradient, down_weight, preferred_element_type=single_float)
    )
    hidden_gradient_narrow = hidden_gradient.astype(brain_float_half)
    up_weight_gradient = jnp.einsum(
        "qgp,qgv->pv",
        second_normalized_narrow,
        hidden_gradient_narrow,
        preferred_element_type=single_float,
    )
    d_attn_part, d_gain_two = norm_back_two(
        jnp.einsum(
            "ixn,on->ixo", hidden_gradient_narrow, up_weight, preferred_element_type=single_float
        )
    )
    d_attn = d_ffn + d_attn_part
    output_gradient_narrow = d_attn.astype(brain_float_half)
    output_weight_gradient = jnp.einsum(
        "nkg,nka->ga",
        output_gradient_narrow,
        attention_context,
        preferred_element_type=single_float,
    )
    context_gradient = jnp.einsum(
        "mbg,gr->mbr", output_gradient_narrow, output_weight, preferred_element_type=single_float
    ).astype(brain_float_half)
    context_gradient = context_gradient.reshape(seq_dev, length, HEADS, HDIM)
    d_values = jnp.einsum(
        "shqk,sqhd->skhd", probs_low, context_gradient, preferred_element_type=single_float
    )
    d_probs = jnp.einsum(
        "sqhd,skhd->shqk", context_gradient, values_all, preferred_element_type=single_float
    )
    d_scores = (attn_probs * (d_probs - jnp.sum(attn_probs * d_probs, -1, keepdims=True))).astype(
        brain_float_half
    )
    d_queries = (
        jnp.einsum("shqk,skhd->sqhd", d_scores, keys_all, preferred_element_type=single_float)
        * 0.125
    )
    d_keys = (
        jnp.einsum("shqk,sqhd->skhd", d_scores, queries, preferred_element_type=single_float)
        * 0.125
    )
    mixed_gradient = jnp.concatenate(
        [
            d_queries.reshape(seq_dev, length, inner),
            d_keys.reshape(seq_dev, length, inner),
            d_values.reshape(seq_dev, length, inner),
        ],
        -1,
    ).astype(brain_float_half)
    query_key_value_gradient = jnp.einsum(
        "rbp,rbg->pg", normalized_narrow, mixed_gradient, preferred_element_type=single_float
    )
    d_embed_part, d_gain_one = norm_back_one(
        jnp.einsum(
            "igp,zp->igz",
            mixed_gradient,
            query_key_value_weight,
            preferred_element_type=single_float,
        )
    )
    d_embedded = d_attn + d_embed_part
    grad_pos = jnp.sum(d_embedded, 0).T
    grad_local = jnp.concatenate(
        [
            query_key_value_gradient,
            output_weight_gradient,
            up_weight_gradient,
            down_weight_gradient,
            grad_pos,
        ],
        1,
    )
    gain_local = jnp.stack([d_gain_one, d_gain_two, d_gain_three])
    dense_grad = lax.psum_scatter(grad_local, ("grp", "row"), scatter_dimension=1, tiled=True)
    row_grads = jnp.concatenate([d_embedded.reshape(tokens, model_width), d_target, neg_grad], 0)
    sent_grads = (
        jnp.zeros((peer_count * capacity, model_width), single_float).at[slot_at].set(row_grads)
    )
    arrived = lax.all_to_all(
        sent_grads.reshape(peer_count, capacity, model_width).astype(jnp.bfloat16),
        "row",
        split_axis=0,
        concat_axis=0,
        tiled=True,
    ).astype(jnp.float32)
    present = asked_ids >= 0
    local_rows = jnp.where(present, asked_ids - row_base, 0).reshape(-1)
    arrived = jnp.where(present[..., None], arrived, 0.0).reshape(-1, model_width)
    owner_grad = jax.ops.segment_sum(arrived, local_rows, num_segments=rows_dev)
    table_full = lax.psum(owner_grad.astype(jnp.bfloat16), "grp").astype(jnp.float32)
    dense_sq = jnp.sum(dense_grad * dense_grad)
    table_sq = jnp.sum(table_full * table_full) / lax.axis_size("grp")
    gain_grad, dense_total, table_total = lax.psum((gain_local, dense_sq, table_sq), ("grp", "row"))
    raw_norm = jnp.sqrt(dense_total + table_total + jnp.sum(gain_grad * gain_grad))
    factor = jnp.minimum(1.0, clip_level / raw_norm)
    table_grad = table_full * factor
    new_accum = table_accum + jnp.mean(table_grad * table_grad, -1)
    new_table = table_weight - rows_rate * table_grad / (jnp.sqrt(new_accum)[:, None] + adam_eps)
    new_dense, new_first, new_second = adam_update(
        dense_weight, dense_first, dense_second, dense_grad * factor, decay_rate, adam_rate
    )
    new_gains, new_gain_first, new_gain_second = adam_update(
        gain_weight, gain_first, gain_second, gain_grad * factor, 0.0, gains_rate
    )
    mean_loss = loss_total / event_total
    return (
        mean_loss,
        raw_norm,
        new_table,
        table_grad,
        new_accum,
        new_table.astype(brain_float_half),
        new_dense,
        new_first,
        new_second,
        new_dense.astype(brain_float_half),
        new_gains,
        new_gain_first,
        new_gain_second,
    )


def solution(mesh):
    return jax.shard_map(
        shards,
        mesh=mesh,
        in_specs=(
            P(("grp", "row"), None),
            P(("grp", "row")),
            P(("grp", "row"), None),
            P(("grp", "row"), None),
            P(("grp", "row")),
            P(("grp", "row")),
            P("row", None),
            P("row"),
            P(None, ("grp", "row")),
            P(None, ("grp", "row")),
            P(None, ("grp", "row")),
            P(),
            P(),
            P(),
        ),
        out_specs=(
            P(),
            P(),
            P("row", None),
            P("row", None),
            P("row"),
            P("row", None),
            P(None, ("grp", "row")),
            P(None, ("grp", "row")),
            P(None, ("grp", "row")),
            P(None, ("grp", "row")),
            P(),
            P(),
            P(),
        ),
        check_vma=False,
    )
```

profile of v0, /device:TPU:0, one launch (start us, length us, event | category | flops | bytes accessed | tf_op | source)
XLA Modules:
  0.0 841.4 jit_solution(8096171434932233010)
XLA Ops:
  10.8 4.7 reduce-window.6
  16.7 20.6 %scatter_custom_fusion = s32[8320]{0:T(1024)S(1)} fusion(s32[4160]{0:T(1024)S(1)} %fusion.57, s32[4160]{0:T(1024)S(1)} %constant_dynamic-update-slice_fusion.1, s32[]{:T(128)} %constant.34.clone.1), kind=kCustom, calls=%fused_computation.133 | custom fusion | bytes 33284 | tf_op jit(solution)/shard_map/scatter | solution.py:102
  38.0 7.4 all-to-all-start
  52.8 24.2 %gather_fusion = bf16[8320,256]{1,0:T(8,128)(2,1)} fusion(bf16[3125,256]{1,0:T(8,128)(2,1)S(1)} %convert_element_type.132, s32[9216]{0:T(1024)S(1)} %pad_clamp_fusion), kind=kCustom, calls=%fused_computation | custom fusion | bytes 8552960 | tf_op jit(solution)/shard_map/gather | solution.py:108
  77.7 5.3 broadcast_select_fusion
  83.0 4.7 all-to-all-start.1
  89.9 99.9 %all-reduce.1 = bf16[1024]{0:T(1024)(128)(2,1)S(1)} all-reduce(bf16[1024]{0:T(1024)(128)(2,1)S(1)} %dynamic-update-slice), channel_id=1, replica_groups=mesh['grp'=2,'row'=16] {'row'}, use_global_device_ids=true, to_apply=%add.1 | all-reduce | flops 1024 | bytes 4096
  191.0 12.5 %gather_fusion.1 = bf16[4160,256]{1,0:T(8,128)(2,1)S(1)} fusion(bf16[8320,256]{1,0:T(8,128)(2,1)} %bitcast.5, s32[5120]{0:T(1024)S(1)} %pad_clamp_fusion.1), kind=kCustom, calls=%fused_computation.1 | custom fusion | bytes 4276480 | tf_op jit(solution)/shard_map/gather | solution.py:112
  205.6 40.4 %all_gather.10 = bf16[1024,256]{1,0:T(8,128)(2,1)} all-gather(bf16[64,256]{1,0:T(8,128)(2,1)S(1)} %slice.84), channel_id=1, replica_groups=mesh['grp'=2,'row'=16] {'row'}, dimensions={0}, use_global_device_ids=true | all-gather | bytes 557056 | tf_op jit(solution)/shard_map/all_gather | solution.py:117
  263.7 19.1 %fusion.72 = (f32[4,8,512]{2,1,0:T(8,128)S(1)}, f32[4,8,512,512]{2,3,1,0:T(8,128)}) fusion(pred[512,512]{0,1:T(8,128)(4,1)S(1)} %iota_compare_fusion, bf16[4,512,8,64]{1,3,2,0:T(8,128)(2,1)} %bitcast.183, bf16[4,512,8,64]{1,3,2,0:T(8,128)(2,1)S(1)} %bitcast.181), kind=kOutput, calls=%fused_computation.173 | convolution fusion | flops 1107296768 | bytes 38076416 | tf_op jit(solution)/shard_map/sub | solution.py:60
  282.8 14.4 %fusion.33 = bf16[4,8,64,512]{3,2,1,0:T(8,128)(2,1)} fusion(bf16[4,512,8,64]{1,3,2,0:T(8,128)(2,1)} %bitcast.193, f32[4,8,512,512]{2,3,1,0:T(8,128)} %get-tuple-element.102, f32[4,8,512]{2,1,0:T(8,128)S(1)} %get-tuple-element.101), kind=kOutput, calls=%fused_computation.78 | convolution fusion | flops 1091567616 | bytes 37814272 | tf_op jit(solution)/shard_map/shqk,skhd->sqhd/dot_general | solution.py:134
  310.7 5.5 subtract_reduce_fusion
  321.2 38.9 %psum.43 = f32[]{:T(128)} all-reduce(f32[]{:T(128)} %get-tuple-element.71), channel_id=1, replica_groups=mesh['grp'=2,'row'=16] {'grp','row'}, use_global_device_ids=true, to_apply=%region_15.16 | all-reduce | flops 1 | bytes 8 | tf_op jit(solution)/shard_map/psum | solution.py:170
  373.8 6.7 fusion.11
  387.8 15.3 %fusion.36 = bf16[4,8,64,512]{3,2,1,0:T(8,128)(2,1)} fusion(bf16[4,512,8,64]{1,3,2,0:T(8,128)(2,1)} %bitcast.196, f32[4,8,512,512]{2,3,1,0:T(8,128)} %get-tuple-element.102, f32[4,8,512]{2,1,0:T(8,128)S(1)} %get-tuple-element.101), kind=kOutput, calls=%fused_computation.79 | convolution fusion | flops 1091567616 | bytes 37814272 | tf_op jit(solution)/shard_map/shqk,sqhd->skhd/dot_general | solution.py:219
  403.1 22.9 %multiply_reduce_fusion = (f32[4,8,512]{2,1,0:T(8,128)S(1)}, f32[4,8,512,512]{2,3,1,0:T(8,128)}) fusion(f32[4,8,512,512]{2,3,1,0:T(8,128)} %get-tuple-element.102, f32[4,8,512]{2,1,0:T(8,128)S(1)} %get-tuple-element.101, bf16[4,512,8,64]{1,3,2,0:T(8,128)(2,1)} %bitcast.197, bf16[4,512,8,64]{1,3,2,0:T(8,128)(2,1)} %bitcast.194), kind=kOutput, calls=%fused_computation.7 | convolution fusion | flops 1098891264 | bytes 71434240 | tf_op jit(solution)/shard_map/sqhd,skhd->shqk/dot_general | solution.py:222
  426.0 27.6 %multiply_convert_fusion = bf16[4,8,512,512]{2,3,1,0:T(8,128)(2,1)} fusion(f32[4,8,512,512]{2,3,1,0:T(8,128)} %get-tuple-element.111, f32[4,8,512]{2,1,0:T(8,128)S(1)} %get-tuple-element.110, f32[4,8,512,512]{2,3,1,0:T(8,128)} %get-tuple-element.102, f32[4,8,512]{2,1,0:T(8,128)S(1)} %get-tuple-element.101), kind=kLoop, calls=%fused_computation.6 | loop fusion | flops 33554432 | bytes 84017152 | tf_op jit(solution)/shard_map/convert_element_type | solution.py:225
  453.6 12.9 %multiply_convert_fusion.3 = bf16[4,8,64,512]{3,2,1,0:T(8,128)(2,1)} fusion(bf16[4,512,8,64]{1,3,2,0:T(8,128)(2,1)} %bitcast.184, bf16[4,8,512,512]{2,3,1,0:T(8,128)(2,1)} %multiply_convert_fusion), kind=kOutput, calls=%fused_computation.43 | convolution fusion | flops 1075838976 | bytes 20971520 | tf_op jit(solution)/shard_map/shqk,sqhd->skhd/dot_general | solution.py:233
  466.5 10.6 %multiply_convert_fusion.4 = bf16[4,8,64,512]{3,2,1,0:T(8,128)(2,1)} fusion(bf16[4,512,8,64]{1,3,2,0:T(8,128)(2,1)} %bitcast.182, bf16[4,8,512,512]{2,3,1,0:T(8,128)(2,1)} %multiply_convert_fusion), kind=kOutput, calls=%fused_computation.44 | convolution fusion | flops 1075838976 | bytes 20971520 | tf_op jit(solution)/shard_map/shqk,skhd->sqhd/dot_general | solution.py:229
  477.1 5.4 all-to-all-start.2
  495.0 5.4 multiply_reduce_fusion.4
  507.2 6.3 fusion.26
  514.6 27.3 %scatter_custom_fusion.1 = f32[8320,256]{1,0:T(8,128)} fusion(s32[4160]{0:T(1024)} %copy-done.28, f32[64,256]{1,0:T(8,128)S(1)} %convert_reduce_fusion, f32[]{:T(128)} %constant.48.clone.1, f32[2048,256]{1,0:T(8,128)} %convert_multiply_fusion.4, f32[2048,256]{1,0:T(8,128)} %bitcast.174, f32[]{:T(128)} %constant.43.clone.1), kind=kCustom, calls=%fused_computation.35 | custom fusion | flops 2129920 | bytes 12780544 | tf_op jit(solution)/shard_map/scatter | solution.py:271
  541.9 5.3 convert_element_type.163
  547.2 6.1 all-to-all-start.3
  559.8 7.6 fusion.41
  568.3 6.0 copy.183
  575.2 63.3 %all-to-all-done.3 = bf16[16,520,256]{2,1,0:T(8,128)(2,1)} async-done(((bf16[16,520,256]{2,1,0:T(8,128)(2,1)}), bf16[16,520,256]{2,1,0:T(8,128)(2,1)}, u32[]{:S(2)}, u32[]{:S(2)}) %all-to-all-start.3) | async-done | bytes 4259872 | tf_op jit(solution)/shard_map/all_to_all | solution.py:273
  638.5 7.1 convert_select_fusion
  645.6 52.6 %scatter_custom_fusion.2 = f32[3125,256]{1,0:T(8,128)S(1)} fusion(s32[8320]{0:T(1024)S(1)} %reshape.563, f32[8320,256]{1,0:T(8,128)} %bitcast.180, f32[]{:T(128)} %constant.43.clone.1), kind=kCustom, calls=%fused_computation.82 | custom fusion | flops 2129920 | bytes 3200512 | tf_op jit(solution)/shard_map/scatter-add | solution.py:283
  701.4 76.3 %all-reduce.5.cloned.1.call-done = bf16[3125,256]{1,0:T(8,128)(2,1)} async-done(((bf16[3125,256]{1,0:T(8,128)(2,1)}), bf16[3125,256]{1,0:T(8,128)(2,1)}) %all-reduce.5.cloned.1.call-update) | async-done | bytes 1600016 | tf_op jit(solution)/shard_map/psum | solution.py:284
  782.0 39.6 %all-reduce.2 = (f32[]{:T(128)}, f32[]{:T(128)}, f32[3,256]{1,0:T(4,128)S(1)}) all-reduce(f32[]{:T(128)} %get-tuple-element.72, f32[]{:T(128)S(6)} %add.230, f32[3,256]{1,0:T(4,128)S(1)} %pad_maximum_fusion.3), channel_id=1, replica_groups=mesh['grp'=2,'row'=16] {'grp','row'}, use_global_device_ids=true, to_apply=%region_13.14 | all-reduce | flops 770 | bytes 6160 | tf_op jit(solution)/shard_map/psum | solution.py:170
  (204 shorter events, 117.0 us)
Async XLA Ops:
  7.2 9.3 %copy-start.44 = (s32[64]{0:T(128)S(1)}, s32[64]{0:T(128)}, u32[]{:S(2)}) copy-start(s32[64]{0:T(128)} %param.18) | copy-start | bytes 772
  16.7 173.2 %copy-start.28 = (s32[4160]{0:T(1024)}, s32[4160]{0:T(1024)S(1)}, u32[]{:S(2)}) copy-start(s32[4160]{0:T(1024)S(1)} %fusion.57) | copy-start | bytes 49924
  38.0 14.1 %all-to-all-start = ((s32[16,1,520]{2,1,0:T(1,128)}), s32[16,1,520]{2,1,0:T(1,128)S(1)}, u32[]{:S(2)}, u32[]{:S(2)}) async-start(s32[16,1,520]{2,1,0:T(1,128)} %all_to_all.15), calls=%async_computation | async-start | bytes 81920 | tf_op jit(solution)/shard_map/all_to_all | solution.py:106
  83.0 4.8 copy-start.21
  83.0 5.5 copy-start.46
  83.0 6.7 copy-start.45
  83.0 106.9 %copy-start.34 = (bf16[4,512]{1,0:T(4,128)(2,1)S(1)}, bf16[4,512]{1,0:T(4,128)(2,1)}, u32[]{:S(2)}) copy-start(bf16[4,512]{1,0:T(4,128)(2,1)} %param.17) | copy-start | bytes 12292
  83.0 107.0 %copy-start.35 = (f32[3,256]{1,0:T(4,128)S(1)}, f32[3,256]{1,0:T(4,128)}, u32[]{:S(2)}) copy-start(f32[3,256]{1,0:T(4,128)} %param.25) | copy-start | bytes 9220
  83.0 108.0 %all-to-all-start.1 = ((bf16[16,520,256]{2,1,0:T(8,128)(2,1)}), bf16[16,520,256]{2,1,0:T(8,128)(2,1)}, u32[]{:S(2)}, u32[]{:S(2)}) async-start(bf16[16,520,256]{2,1,0:T(8,128)(2,1)} %broadcast_select_fusion), calls=%async_computation.1 | async-start | bytes 8519680 | tf_op jit(solution)/shard_map/all_to_all | solution.py:110
  87.7 102.3 %all-gather.2.cloned.1.call-start = ((), (), s32[]{:S(2)}) async-start(), calls=%async_computation.5 | async-start | bytes 2433024 | tf_op jit(solution)/shard_map/all_gather | solution.py:88
  190.0 56.1 %copy-start.37 = (f32[1,256]{1,0:T(1,128)}, f32[1,256]{1,0:T(1,128)S(1)}, u32[]{:S(2)}) copy-start(f32[1,256]{1,0:T(1,128)S(1)} %get-tuple-element.100) | copy-start | bytes 3076
  191.0 106.2 %copy-start.9 = (f32[512,256]{1,0:T(8,128)}, f32[512,256]{1,0:T(8,128)S(1)}, u32[]{:S(2)}) copy-start(f32[512,256]{1,0:T(8,128)S(1)} %convert_bitcast_fusion) | copy-start | bytes 1572868
  203.6 42.5 %copy-start.2 = (bf16[4160,256]{1,0:T(8,128)(2,1)}, bf16[4160,256]{1,0:T(8,128)(2,1)S(1)}, u32[]{:S(2)}) copy-start(bf16[4160,256]{1,0:T(8,128)(2,1)S(1)} %gather_fusion.1) | copy-start | bytes 6389764
  205.6 43.7 %copy-start.29 = (f32[4,512]{1,0:T(4,128)}, f32[4,512]{1,0:T(4,128)S(1)}, u32[]{:S(2)}) copy-start(f32[4,512]{1,0:T(4,128)S(1)} %add.216) | copy-start | bytes 24580
  205.6 43.7 %copy-start.31 = (f32[4,512]{1,0:T(4,128)}, f32[4,512]{1,0:T(4,128)S(1)}, u32[]{:S(2)}) copy-start(f32[4,512]{1,0:T(4,128)S(1)} %rsqrt.30) | copy-start | bytes 24580
  255.0 8.7 %copy-start.15 = (bf16[4,512,512]{1,2,0:T(8,128)(2,1)}, bf16[4,512,512]{1,2,0:T(8,128)(2,1)S(1)}, u32[]{:S(2)}) copy-start(bf16[4,512,512]{1,2,0:T(8,128)(2,1)S(1)} %copy.151) | copy-start | bytes 6291460
  302.9 4.5 copy-start.16
  365.4 8.0 slice-start
  367.5 5.9 slice-start.1
  369.0 13.8 %copy-start.7 = (f32[2048,256]{1,0:T(8,128)}, f32[2048,256]{1,0:T(8,128)S(1)}, u32[]{:S(2)}) copy-start(f32[2048,256]{1,0:T(8,128)S(1)} %convolution_add_fusion) | copy-start | bytes 6291460
  477.1 36.4 %all-to-all-start.2 = ((bf16[16,64,256]{2,1,0:T(8,128)(2,1)}), bf16[16,64,256]{2,1,0:T(8,128)(2,1)}, u32[]{:S(2)}, u32[]{:S(2)}) async-start(bf16[16,64,256]{2,1,0:T(8,128)(2,1)} %bitcast.39), calls=%async_computation.2 | async-start | bytes 1048576 | tf_op jit(solution)/shard_map/all_to_all | solution.py:28
  495.0 5.5 copy-start.30
  495.0 5.5 copy-start.1
  547.2 91.3 %all-to-all-start.3 = ((bf16[16,520,256]{2,1,0:T(8,128)(2,1)}), bf16[16,520,256]{2,1,0:T(8,128)(2,1)}, u32[]{:S(2)}, u32[]{:S(2)}) async-start(bf16[16,520,256]{2,1,0:T(8,128)(2,1)} %bitcast.179), calls=%async_computation.3 | async-start | bytes 8519680 | tf_op jit(solution)/shard_map/all_to_all | solution.py:273
  553.3 146.3 %reduce-scatter.4.cloned.1.call-start = ((), (), s32[]{:S(2)}) async-start(), calls=%async_computation.7 | async-start | bytes 4866048
  574.3 64.2 %copy-start.27 = (pred[16,520]{1,0:T(8,128)(4,1)S(1)}, pred[16,520]{1,0:T(8,128)(4,1)}, u32[]{:S(2)}) copy-start(pred[16,520]{1,0:T(8,128)(4,1)} %copy-done.26) | copy-start | bytes 24964
  574.3 203.4 %all-reduce.5.cloned.1.call-start = ((), (), s32[]{:S(2)}) async-start(), calls=%async_computation.6 | async-start | bytes 3203072 | tf_op jit(solution)/shard_map/psum | solution.py:284
  699.6 125.3 %copy-start.36 = (f32[3,256]{1,0:T(4,128)S(1)}, f32[3,256]{1,0:T(4,128)}, u32[]{:S(2)}) copy-start(f32[3,256]{1,0:T(4,128)} %param.25) | copy-start | bytes 9220
  699.6 125.3 %copy-start.40 = (f32[3,256]{1,0:T(4,128)S(1)}, f32[3,256]{1,0:T(4,128)}, u32[]{:S(2)}) copy-start(f32[3,256]{1,0:T(4,128)} %param.26) | copy-start | bytes 9220
  699.6 125.3 %copy-start.41 = (f32[3,256]{1,0:T(4,128)S(1)}, f32[3,256]{1,0:T(4,128)}, u32[]{:S(2)}) copy-start(f32[3,256]{1,0:T(4,128)} %param.27) | copy-start | bytes 9220
  777.7 47.8 %copy-start.17 = (bf16[3125,256]{1,0:T(8,128)(2,1)S(1)}, bf16[3125,256]{1,0:T(8,128)(2,1)}, u32[]{:S(2)}) copy-start(bf16[3125,256]{1,0:T(8,128)(2,1)} %all-reduce.5.cloned.1.call-done) | copy-start | bytes 4800004
  826.1 5.5 copy-start.12
  (24 other events, 59.5 us)
Sparse Core Ops, SparseCore 0:
  92.0 97.0 all-gather.1
  574.4 113.9 reduce-scatter.3
  699.7 77.9 all-reduce.4
where the time goes:
time: 849 us; the launch traced here: 841 us
  blocking collectives  219 us (26%)
  other arithmetic  171 us (20%)
  matrix products  154 us (18%)
  waiting for transfers between devices  144 us (17%)
  local copies, waits for them, and re-layouts  107 us (13%)
  starting transfers between devices  23.7 us (3%)
  between operations  22.5 us (3%)
    unnamed x1, blocking collectives  99.9 us
    psum x2, blocking collectives, shards(): lax.psum((loss_local, event_local), ('grp', 'row'))  78.5 us
    psum x1, waiting for transfers between devices, shards(): lax.psum(owner_grad.astype(jnp.bfloat16), 'grp').astype(jnp.float32)  76.3 us
    all_to_all x1, waiting for transfers between devices, shards(): lax.all_to_all(sent_grads.reshape(peer_count, capacity, model_width).asty...  63.3 us
    scatter-add x1, other arithmetic, shards(): owner_grad = jax.ops.segment_sum(arrived, local_rows, num_segments=rows_dev)  52.6 us
    all_gather x1, blocking collectives, shards(): lax.all_gather(own_negatives, 'row', axis=0, tiled=True)  40.4 us
    convert_element_type x1, other arithmetic, shards(): (attn_probs * (d_probs - jnp.sum(attn_probs * d_probs, -1, keepdims=True)...  27.6 us
    scatter x1, other arithmetic, shards(): jnp.zeros((peer_count * capacity, model_width), single_float).at[slot_at]  27.3 us
  transfers between devices with their start and end apart: 7, of which 3 were waited for; matrix products, arithmetic and copies ran while one was open for 14% of the time, Pallas kernels for 0%

commit v1 on v0

--- a/solution.py
+++ b/solution.py
@@ -15,6 +15,23 @@
 beta_two = 0.999
 adam_eps = 1e-08
 decay_rate = 0.01
+
+
+def in_order(pieces, dim):
+    pieces = jnp.moveaxis(pieces, 0, dim)
+    dims = pieces.shape
+    return pieces.reshape(*dims[:dim], dims[dim] * dims[dim + 1], *dims[dim + 2 :])
+
+
+def gather_around(value, axis, dim):
+    count = lax.axis_size(axis)
+    right = [(i, (i + 1) % count) for i in range(count)]
+    blocks = [value]
+    while len(blocks) < count:
+        blocks.append(lax.ppermute(blocks[-1], axis, right))
+    place = lax.axis_index(axis)
+    blocks = jnp.stack(blocks)[(place - jnp.arange(count)) % count]
+    return in_order(blocks, dim)
 
 
 def in_blocks(array, dim, devices):
@@ -114,7 +131,7 @@
     target_rows = picked[tokens : 2 * tokens]
     own_negatives = picked[2 * tokens :]
     neg_rows, neg_bias = (
-        lax.all_gather(own_negatives, "row", axis=0, tiled=True),
+        gather_around(own_negatives, "row", 0),
         lax.all_gather(negative_logq, "row", axis=0, tiled=True),
     )
     embedded_tokens = hist_rows.astype(single_float) + pos_rows[None]

time: 849 us -> 911 us (1.073)
  waiting for transfers between devices: 144 us -> 218 us
  blocking collectives: 219 us -> 177 us
  starting transfers between devices: 23.7 us -> 42.2 us
  local copies, waits for them, and re-layouts: 107 us -> 120 us
    ppermute x0 -> x15, waiting for transfers between devices: none -> 73.5 us  [gather_around(): blocks.append(lax.ppermute(blocks[-1], axis, right))]
    all_gather x1 -> x0, blocking collectives: 40.4 us -> none  [shards(): lax.all_gather(own_negatives, 'row', axis=0, tiled=True)]
    ppermute x0 -> x15, starting transfers between devices: none -> 17.3 us  [gather_around(): blocks.append(lax.ppermute(blocks[-1], axis, right))]
    unnamed x112 -> x129, local copies, waits for them, and re-layouts: 18.7 us -> 28.6 us
  transfers between devices with their start and end apart: 7 -> 22, of which waited for: 3 -> 17; matrix products, arithmetic and copies ran while one was open for 14% -> 21% of each run, Pallas kernels for 0% -> 0%
where the time goes in v1:
time: 911 us; the launch traced here: 904 us
  waiting for transfers between devices  218 us (24%)
  blocking collectives  177 us (19%)
  other arithmetic  169 us (19%)
  matrix products  155 us (17%)
  local copies, waits for them, and re-layouts  120 us (13%)
  starting transfers between devices  42.2 us (5%)
  between operations  22.5 us (2%)
    unnamed x1, blocking collectives  99.9 us
    psum x1, waiting for transfers between devices, shards(): lax.psum(owner_grad.astype(jnp.bfloat16), 'grp').astype(jnp.float32)  77.2 us
    psum x2, blocking collectives, shards(): lax.psum((loss_local, event_local), ('grp', 'row'))  76.8 us
    ppermute x15, waiting for transfers between devices, gather_around(): blocks.append(lax.ppermute(blocks[-1], axis, right))  73.5 us
    all_to_all x1, waiting for transfers between devices, shards(): lax.all_to_all(sent_grads.reshape(peer_count, capacity, model_width).asty...  62.8 us
    scatter-add x1, other arithmetic, shards(): owner_grad = jax.ops.segment_sum(arrived, local_rows, num_segments=rows_dev)  52.6 us
    unnamed x129, local copies, waits for them, and re-layouts  28.6 us
    convert_element_type x1, other arithmetic, shards(): (attn_probs * (d_probs - jnp.sum(attn_probs * d_probs, -1, keepdims=True)...  27.6 us
  transfers between devices with their start and end apart: 22, of which 17 were waited for; matrix products, arithmetic and copies ran while one was open for 21% of the time, Pallas kernels for 0%

profile of v1, /device:TPU:0, one launch (start us, length us, event | category | flops | bytes accessed | tf_op | source)
XLA Modules:
  0.0 903.5 jit_solution(14629749971432632154)
XLA Ops:
  16.7 20.6 %scatter_custom_fusion = s32[8320]{0:T(1024)S(1)} fusion(s32[4160]{0:T(1024)S(1)} %fusion.57, s32[4160]{0:T(1024)S(1)} %constant_dynamic-update-slice_fusion.17, s32[]{:T(128)} %constant.36.clone.1), kind=kCustom, calls=%fused_computation.151 | custom fusion | bytes 33284 | tf_op jit(solution)/shard_map/scatter | solution.py:119
  38.0 7.4 all-to-all-start
  52.8 24.2 %gather_fusion = bf16[8320,256]{1,0:T(8,128)(2,1)} fusion(bf16[3125,256]{1,0:T(8,128)(2,1)S(1)} %convert_element_type.132, s32[9216]{0:T(1024)S(1)} %pad_clamp_fusion), kind=kCustom, calls=%fused_computation | custom fusion | bytes 8552960 | tf_op jit(solution)/shard_map/gather | solution.py:125
  89.9 99.9 %all-reduce.1 = bf16[1024]{0:T(1024)(128)(2,1)S(1)} all-reduce(bf16[1024]{0:T(1024)(128)(2,1)S(1)} %dynamic-update-slice), channel_id=1, replica_groups=mesh['grp'=2,'row'=16] {'row'}, use_global_device_ids=true, to_apply=%add.1 | all-reduce | flops 1024 | bytes 4096
  191.1 12.5 %gather_fusion.1 = bf16[4160,256]{1,0:T(8,128)(2,1)S(1)} fusion(bf16[8320,256]{1,0:T(8,128)(2,1)} %bitcast.5, s32[5120]{0:T(1024)S(1)} %pad_clamp_fusion.1), kind=kCustom, calls=%fused_computation.1 | custom fusion | bytes 4276480 | tf_op jit(solution)/shard_map/gather | solution.py:129
  205.6 15.0 %collective-permute-start = (bf16[64,256]{1,0:T(8,128)(2,1)S(1)}, bf16[64,256]{1,0:T(8,128)(2,1)S(1)}, u32[]{:S(2)}, u32[]{:S(2)}) collective-permute-start(bf16[64,256]{1,0:T(8,128)(2,1)S(1)} %slice.86), channel_id=1, source_target_pairs={{0,1},{1,2},{2,3},{3,4},{4,5},{5,6},{6,7},{7,8},{8,9},{9,10},{10,1... | collective-permute-start | bytes 98312 | tf_op jit(solution)/shard_map/ppermute | solution.py:31
  238.3 19.1 %fusion.74 = (f32[4,8,512]{2,1,0:T(8,128)S(1)}, f32[4,8,512,512]{2,3,1,0:T(8,128)}) fusion(pred[512,512]{0,1:T(8,128)(4,1)S(1)} %iota_compare_fusion, bf16[4,512,8,64]{1,3,2,0:T(8,128)(2,1)} %bitcast.218, bf16[4,512,8,64]{1,3,2,0:T(8,128)(2,1)S(1)} %bitcast.216), kind=kOutput, calls=%fused_computation.197 | convolution fusion | flops 1107296768 | bytes 38076416 | tf_op jit(solution)/shard_map/sub | solution.py:77
  257.4 14.7 %fusion.33 = bf16[4,8,64,512]{3,2,1,0:T(8,128)(2,1)} fusion(bf16[4,512,8,64]{1,3,2,0:T(8,128)(2,1)} %bitcast.230, f32[4,8,512,512]{2,3,1,0:T(8,128)} %get-tuple-element.102, f32[4,8,512]{2,1,0:T(8,128)S(1)} %get-tuple-element.101), kind=kOutput, calls=%fused_computation.79 | convolution fusion | flops 1091567616 | bytes 37814272 | tf_op jit(solution)/shard_map/shqk,skhd->sqhd/dot_general | solution.py:151
  292.4 5.4 collective-permute-done.2
  298.5 5.4 collective-permute-done.3
  304.5 5.4 collective-permute-done.4
  346.8 5.4 collective-permute-done.11
  373.4 5.5 subtract_reduce_fusion
  383.9 37.2 %psum.43 = f32[]{:T(128)} all-reduce(f32[]{:T(128)} %get-tuple-element.71), channel_id=1, replica_groups=mesh['grp'=2,'row'=16] {'grp','row'}, use_global_device_ids=true, to_apply=%region_15.16 | all-reduce | flops 1 | bytes 8 | tf_op jit(solution)/shard_map/psum | solution.py:187
  434.9 6.7 fusion.11
  448.8 15.3 %fusion.36 = bf16[4,8,64,512]{3,2,1,0:T(8,128)(2,1)} fusion(bf16[4,512,8,64]{1,3,2,0:T(8,128)(2,1)} %bitcast.233, f32[4,8,512,512]{2,3,1,0:T(8,128)} %get-tuple-element.102, f32[4,8,512]{2,1,0:T(8,128)S(1)} %get-tuple-element.101), kind=kOutput, calls=%fused_computation.80 | convolution fusion | flops 1091567616 | bytes 37814272 | tf_op jit(solution)/shard_map/shqk,sqhd->skhd/dot_general | solution.py:236
  464.1 22.7 %multiply_reduce_fusion = (f32[4,8,512]{2,1,0:T(8,128)S(1)}, f32[4,8,512,512]{2,3,1,0:T(8,128)}) fusion(f32[4,8,512,512]{2,3,1,0:T(8,128)} %get-tuple-element.102, f32[4,8,512]{2,1,0:T(8,128)S(1)} %get-tuple-element.101, bf16[4,512,8,64]{1,3,2,0:T(8,128)(2,1)} %bitcast.234, bf16[4,512,8,64]{1,3,2,0:T(8,128)(2,1)} %bitcast.231), kind=kOutput, calls=%fused_computation.8 | convolution fusion | flops 1098891264 | bytes 71434240 | tf_op jit(solution)/shard_map/sqhd,skhd->shqk/dot_general | solution.py:239
  486.8 27.6 %multiply_convert_fusion = bf16[4,8,512,512]{2,3,1,0:T(8,128)(2,1)} fusion(f32[4,8,512,512]{2,3,1,0:T(8,128)} %get-tuple-element.111, f32[4,8,512]{2,1,0:T(8,128)S(1)} %get-tuple-element.110, f32[4,8,512,512]{2,3,1,0:T(8,128)} %get-tuple-element.102, f32[4,8,512]{2,1,0:T(8,128)S(1)} %get-tuple-element.101), kind=kLoop, calls=%fused_computation.7 | loop fusion | flops 33554432 | bytes 84017152 | tf_op jit(solution)/shard_map/convert_element_type | solution.py:242
  514.4 12.9 %multiply_convert_fusion.3 = bf16[4,8,64,512]{3,2,1,0:T(8,128)(2,1)} fusion(bf16[4,512,8,64]{1,3,2,0:T(8,128)(2,1)} %bitcast.219, bf16[4,8,512,512]{2,3,1,0:T(8,128)(2,1)} %multiply_convert_fusion), kind=kOutput, calls=%fused_computation.44 | convolution fusion | flops 1075838976 | bytes 20971520 | tf_op jit(solution)/shard_map/shqk,sqhd->skhd/dot_general | solution.py:250
  527.3 10.6 %multiply_convert_fusion.4 = bf16[4,8,64,512]{3,2,1,0:T(8,128)(2,1)} fusion(bf16[4,512,8,64]{1,3,2,0:T(8,128)(2,1)} %bitcast.217, bf16[4,8,512,512]{2,3,1,0:T(8,128)(2,1)} %multiply_convert_fusion), kind=kOutput, calls=%fused_computation.45 | convolution fusion | flops 1075838976 | bytes 20971520 | tf_op jit(solution)/shard_map/shqk,skhd->sqhd/dot_general | solution.py:246
  537.9 6.5 all-to-all-start.2
  556.9 5.4 multiply_reduce_fusion.4
  569.0 6.3 fusion.26
  576.5 27.3 %scatter_custom_fusion.1 = f32[8320,256]{1,0:T(8,128)} fusion(s32[4160]{0:T(1024)} %copy-done.29, f32[64,256]{1,0:T(8,128)S(1)} %convert_reduce_fusion, f32[]{:T(128)} %constant.50.clone.1, f32[2048,256]{1,0:T(8,128)} %convert_multiply_fusion.4, f32[2048,256]{1,0:T(8,128)} %bitcast.209, f32[]{:T(128)} %constant.45.clone.1), kind=kCustom, calls=%fused_computation.36 | custom fusion | flops 2129920 | bytes 12780544 | tf_op jit(solution)/shard_map/scatter | solution.py:288
  609.1 6.1 all-to-all-start.3
  621.7 7.6 fusion.41
  630.2 6.0 copy.183
  637.1 62.8 %all-to-all-done.3 = bf16[16,520,256]{2,1,0:T(8,128)(2,1)} async-done(((bf16[16,520,256]{2,1,0:T(8,128)(2,1)}), bf16[16,520,256]{2,1,0:T(8,128)(2,1)}, u32[]{:S(2)}, u32[]{:S(2)}) %all-to-all-start.3) | async-done | bytes 4259872 | tf_op jit(solution)/shard_map/all_to_all | solution.py:290
  699.9 7.1 convert_select_fusion
  706.9 52.6 %scatter_custom_fusion.2 = f32[3125,256]{1,0:T(8,128)S(1)} fusion(s32[8320]{0:T(1024)S(1)} %reshape.624, f32[8320,256]{1,0:T(8,128)} %bitcast.215, f32[]{:T(128)} %constant.45.clone.1), kind=kCustom, calls=%fused_computation.83 | custom fusion | flops 2129920 | bytes 3200512 | tf_op jit(solution)/shard_map/scatter-add | solution.py:300
  762.7 77.2 %all-reduce.5.cloned.1.call-done = bf16[3125,256]{1,0:T(8,128)(2,1)} async-done(((bf16[3125,256]{1,0:T(8,128)(2,1)}), bf16[3125,256]{1,0:T(8,128)(2,1)}) %all-reduce.5.cloned.1.call-update) | async-done | bytes 1600016 | tf_op jit(solution)/shard_map/psum | solution.py:301
  844.1 39.6 %all-reduce.2 = (f32[]{:T(128)}, f32[]{:T(128)}, f32[3,256]{1,0:T(4,128)S(1)}) all-reduce(f32[]{:T(128)} %get-tuple-element.72, f32[]{:T(128)S(6)} %add.255, f32[3,256]{1,0:T(4,128)S(1)} %pad_maximum_fusion.3), channel_id=1, replica_groups=mesh['grp'=2,'row'=16] {'grp','row'}, use_global_device_ids=true, to_apply=%region_13.14 | all-reduce | flops 770 | bytes 6160 | tf_op jit(solution)/shard_map/psum | solution.py:187
  (254 shorter events, 203.1 us)
Async XLA Ops:
  16.7 173.2 %copy-start.29 = (s32[4160]{0:T(1024)}, s32[4160]{0:T(1024)S(1)}, u32[]{:S(2)}) copy-start(s32[4160]{0:T(1024)S(1)} %fusion.57) | copy-start | bytes 49924
  38.0 14.1 %all-to-all-start = ((s32[16,1,520]{2,1,0:T(1,128)}), s32[16,1,520]{2,1,0:T(1,128)S(1)}, u32[]{:S(2)}, u32[]{:S(2)}) async-start(s32[16,1,520]{2,1,0:T(1,128)} %all_to_all.15), calls=%async_computation | async-start | bytes 81920 | tf_op jit(solution)/shard_map/all_to_all | solution.py:123
  83.0 106.9 %copy-start.35 = (bf16[4,512]{1,0:T(4,128)(2,1)S(1)}, bf16[4,512]{1,0:T(4,128)(2,1)}, u32[]{:S(2)}) copy-start(bf16[4,512]{1,0:T(4,128)(2,1)} %param.17) | copy-start | bytes 12292
  83.0 107.0 %copy-start.36 = (f32[3,256]{1,0:T(4,128)S(1)}, f32[3,256]{1,0:T(4,128)}, u32[]{:S(2)}) copy-start(f32[3,256]{1,0:T(4,128)} %param.25) | copy-start | bytes 9220
  83.0 108.1 %all-to-all-start.1 = ((bf16[16,520,256]{2,1,0:T(8,128)(2,1)}), bf16[16,520,256]{2,1,0:T(8,128)(2,1)}, u32[]{:S(2)}, u32[]{:S(2)}) async-start(bf16[16,520,256]{2,1,0:T(8,128)(2,1)} %broadcast_select_fusion), calls=%async_computation.1 | async-start | bytes 8519680 | tf_op jit(solution)/shard_map/all_to_all | solution.py:127
  87.7 102.4 %all-gather.2.cloned.1.call-start = ((), (), s32[]{:S(2)}) async-start(), calls=%async_computation.5 | async-start | bytes 2433024 | tf_op jit(solution)/shard_map/all_gather | solution.py:105
  190.0 30.6 %copy-start.38 = (f32[1,256]{1,0:T(1,128)}, f32[1,256]{1,0:T(1,128)S(1)}, u32[]{:S(2)}) copy-start(f32[1,256]{1,0:T(1,128)S(1)} %get-tuple-element.100) | copy-start | bytes 3076
  191.0 81.1 %copy-start.10 = (f32[512,256]{1,0:T(8,128)}, f32[512,256]{1,0:T(8,128)S(1)}, u32[]{:S(2)}) copy-start(f32[512,256]{1,0:T(8,128)S(1)} %convert_bitcast_fusion) | copy-start | bytes 1572868
  205.6 80.1 %collective-permute-start = (bf16[64,256]{1,0:T(8,128)(2,1)S(1)}, bf16[64,256]{1,0:T(8,128)(2,1)S(1)}, u32[]{:S(2)}, u32[]{:S(2)}) collective-permute-start(bf16[64,256]{1,0:T(8,128)(2,1)S(1)} %slice.86), channel_id=1, source_target_pairs={{0,1},{1,2},{2,3},{3,4},{4,5},{5,6},{6,7},{7,8},{8,9},{9,10},{10,1... | collective-permute-start | bytes 98312 | tf_op jit(solution)/shard_map/ppermute | solution.py:31
  285.8 6.0 collective-permute-start.1
  291.8 6.0 collective-permute-start.2
  297.8 6.0 collective-permute-start.3
  303.9 6.0 collective-permute-start.4
  309.9 6.0 collective-permute-start.5
  316.0 6.0 collective-permute-start.6
  322.0 6.0 collective-permute-start.7
  328.0 6.0 collective-permute-start.8
  334.1 6.0 collective-permute-start.9
  340.1 6.0 collective-permute-start.10
  346.1 6.0 collective-permute-start.11
  352.2 6.0 collective-permute-start.12
  358.2 6.0 collective-permute-start.13
  364.3 6.0 collective-permute-start.14
  537.9 37.5 %all-to-all-start.2 = ((bf16[16,64,256]{2,1,0:T(8,128)(2,1)}), bf16[16,64,256]{2,1,0:T(8,128)(2,1)}, u32[]{:S(2)}, u32[]{:S(2)}) async-start(bf16[16,64,256]{2,1,0:T(8,128)(2,1)} %bitcast.57), calls=%async_computation.2 | async-start | bytes 1048576 | tf_op jit(solution)/shard_map/all_to_all | solution.py:45
  609.1 90.8 %all-to-all-start.3 = ((bf16[16,520,256]{2,1,0:T(8,128)(2,1)}), bf16[16,520,256]{2,1,0:T(8,128)(2,1)}, u32[]{:S(2)}, u32[]{:S(2)}) async-start(bf16[16,520,256]{2,1,0:T(8,128)(2,1)} %bitcast.214), calls=%async_computation.3 | async-start | bytes 8519680 | tf_op jit(solution)/shard_map/all_to_all | solution.py:290
  615.2 145.7 %reduce-scatter.4.cloned.1.call-start = ((), (), s32[]{:S(2)}) async-start(), calls=%async_computation.7 | async-start | bytes 4866048
  636.2 63.7 %copy-start.28 = (pred[16,520]{1,0:T(8,128)(4,1)S(1)}, pred[16,520]{1,0:T(8,128)(4,1)}, u32[]{:S(2)}) copy-start(pred[16,520]{1,0:T(8,128)(4,1)} %copy-done.27) | copy-start | bytes 24964
  636.2 203.7 %all-reduce.5.cloned.1.call-start = ((), (), s32[]{:S(2)}) async-start(), calls=%async_computation.6 | async-start | bytes 3203072 | tf_op jit(solution)/shard_map/psum | solution.py:301
  760.9 126.1 %copy-start.37 = (f32[3,256]{1,0:T(4,128)S(1)}, f32[3,256]{1,0:T(4,128)}, u32[]{:S(2)}) copy-start(f32[3,256]{1,0:T(4,128)} %param.25) | copy-start | bytes 9220
  760.9 126.1 %copy-start.41 = (f32[3,256]{1,0:T(4,128)S(1)}, f32[3,256]{1,0:T(4,128)}, u32[]{:S(2)}) copy-start(f32[3,256]{1,0:T(4,128)} %param.26) | copy-start | bytes 9220
  760.9 126.2 %copy-start.42 = (f32[3,256]{1,0:T(4,128)S(1)}, f32[3,256]{1,0:T(4,128)}, u32[]{:S(2)}) copy-start(f32[3,256]{1,0:T(4,128)} %param.27) | copy-start | bytes 9220
  839.9 47.8 %copy-start.18 = (bf16[3125,256]{1,0:T(8,128)(2,1)S(1)}, bf16[3125,256]{1,0:T(8,128)(2,1)}, u32[]{:S(2)}) copy-start(bf16[3125,256]{1,0:T(8,128)(2,1)} %all-reduce.5.cloned.1.call-done) | copy-start | bytes 4800004
  (40 other events, 200.7 us)
Sparse Core Ops, SparseCore 0:
  92.0 97.0 all-gather.1
  636.3 114.3 reduce-scatter.3
  761.1 78.7 all-reduce.4
